TPU v7x, 256 devices: a whole 4x4x8 slice. The times are simulated.
256 devices in a mesh: tm: 64 (over z, x, core), blk: 4 (over y).
Axes of the slice: x: 4, y: 4, z: 8, core: 2. Of those that a mesh axis runs over, the one named last changes fastest.
Arguments:
- prior_mean: float32 [512], replicated, may hold values from -6 to 6
- after_mean: float32 [512], replicated, may hold values from -6 to 6
- filter_map: float32 [128, 512, 512], P('tm', 'blk'), may hold values from -1 to 1.5
- smoother_gain: float32 [128, 512, 512], P('tm', 'blk'), may hold values from -1 to 1.5
- smoother_map: float32 [128, 512, 512], P('tm', 'blk'), may hold values from -1 to 1.5
- obs_gain: float32 [128, 512, 128], P('tm', 'blk'), may hold values from -0.5 to 0.5
- observations: float32 [128, 128], P('tm'), may hold values from -6 to 6
Outputs:
- filtered: float32 [128, 512], P('tm', 'blk')
- smoothed: float32 [128, 512], P('tm', 'blk')
All inputs are finite; a program needn't handle non-finite values.
Results may differ from a plain program's by a relative error of at most 0.0003.
Values sent between devices are 32-bit elements; how exact they have to be, the bound alone decides.
A program may use at most 128 MiB of HBM per device.

v0:
```python
import jax
import jax.numpy as jnp
from jax import lax
from jax.sharding import Mesh
from jax.sharding import PartitionSpec as P

TM = ("tm_0", "tm_1", "tm_2")


def neutral_like(value, identity):
    return jax.tree.map(
        lambda part, zero: jnp.zeros_like(part) + jnp.asarray(zero, part.dtype), value, identity
    )


def prefix_by_axis(value, axes, combine, identity, reverse):
    before = start = neutral_like(value, identity)
    so_far = value
    for axis in reversed(axes):
        length, index = (lax.axis_size(axis), lax.axis_index(axis))
        pieces = jax.tree.map(lambda part: lax.all_gather(part, axis), so_far)
        inside, so_far = (start, start)
        for k in reversed(range(length)) if reverse else range(length):
            passed = k > index if reverse else k < index
            so_far = combine(so_far, jax.tree.map(lambda part: part[k], pieces))
            inside = jax.tree.map(lambda new, old: jnp.where(passed, new, old), so_far, inside)
        before = combine(inside, before)
    return before


def chain_combine(earlier, later):
    highest = lax.Precision.HIGHEST
    joined_map = jnp.dot(later[0], earlier[0], precision=highest)
    joined_offset = jnp.dot(later[0], earlier[1], precision=highest) + later[1]
    return (joined_map, joined_offset)


def shards(prior_mean, after_mean, filter_map, smoother_gain, smoother_map, obs_gain, observations):
    highest = lax.Precision.HIGHEST
    steps = filter_map.shape[0]
    rows = filter_map.shape[1]
    width = filter_map.shape[2]
    first_row = lax.axis_index("blk") * rows
    drive_rows = jnp.einsum("tro,to->tr", obs_gain, observations, precision=highest)
    full_filter, full_gain, drive = (
        lax.all_gather(filter_map, "blk", axis=1, tiled=True),
        lax.all_gather(smoother_gain, "blk", axis=1, tiled=True),
        lax.all_gather(drive_rows, "blk", axis=1, tiled=True),
    )
    identity = jnp.eye(width, dtype=jnp.float32)
    nothing = jnp.zeros((width,), jnp.float32)
    offset = nothing
    for index in range(steps):
        offset = jnp.dot(full_filter[index], offset, precision=highest) + drive[index]
    composite = full_filter[steps - 1]
    index = 0
    composite = jnp.dot(composite, full_filter[index], precision=highest)
    total = prefix_by_axis((composite, offset), TM, chain_combine, (identity, nothing), False)
    entering = jnp.dot(total[0], prior_mean, precision=highest) + total[1]
    current = entering
    filtered_list = []
    for index in range(steps):
        current = jnp.dot(full_filter[index], current, precision=highest) + drive[index]
        filtered_list.append(current)
    filtered_full = jnp.stack(filtered_list, axis=0)
    filtered_rows = lax.dynamic_slice_in_dim(filtered_full, first_row, rows, 1)
    pulled_rows = jnp.einsum("trk,tk->tr", smoother_map, filtered_full, precision=highest)
    pulled = lax.all_gather(pulled_rows, "blk", axis=1, tiled=True)
    offset = nothing
    for index in range(steps - 1, -1, -1):
        offset = jnp.dot(full_gain[index], offset, precision=highest) + pulled[index]
    composite = full_gain[0]
    index = 1
    composite = jnp.dot(composite, full_gain[index], precision=highest)
    total = prefix_by_axis((composite, offset), TM, chain_combine, (identity, nothing), True)
    leaving = jnp.dot(total[0], after_mean, precision=highest) + total[1]
    current = leaving
    smoothed_list = []
    for index in range(steps - 1, -1, -1):
        current = jnp.dot(full_gain[index], current, precision=highest) + pulled[index]
        smoothed_list.append(current)
    smoothed_full = jnp.stack(smoothed_list[::-1], axis=0)
    smoothed_rows = lax.dynamic_slice_in_dim(smoothed_full, first_row, rows, 1)
    return (filtered_rows, smoothed_rows)


def solution(mesh):
    torus = Mesh(mesh.devices.reshape(8, 4, 2, mesh.shape["blk"]), ("tm_0", "tm_1", "tm_2", "blk"))
    in_specs = (
        P(),
        P(),
        P(TM, "blk", None),
        P(TM, "blk", None),
        P(TM, "blk", None),
        P(TM, "blk", None),
        P(TM, None),
    )
    out_specs = (P(TM, "blk"), P(TM, "blk"))
    return jax.shard_map(
        shards, mesh=torus, in_specs=in_specs, out_specs=out_specs, check_vma=False
    )
```

profile of v0, /device:TPU:1, one launch (start us, length us, event | category | flops | bytes accessed | tf_op | source)
XLA Modules:
  0.0 462.8 jit_solution(7283257458123513231)
XLA Ops:
  8.7 38.1 %all-gather.27.cloned.1.call-done = f32[2,512,512]{2,1,0:T(8,128)} async-done(((f32[2,128,512]{2,1,0:T(8,128)}), f32[2,512,512]{2,1,0:T(8,128)}) %all-gather.27.cloned.1.call-update) | async-done | bytes 2097168 | tf_op jit(solution)/shard_map/all_gather | solution.py:46
  46.8 4.4 fusion.142
  51.2 30.8 %all-gather.29.cloned.1.call-done = f32[2,512,512]{2,1,0:T(8,128)} async-done(((f32[2,128,512]{2,1,0:T(8,128)}), f32[2,512,512]{2,1,0:T(8,128)}) %all-gather.29.cloned.1.call-update) | async-done | bytes 2097168 | tf_op jit(solution)/shard_map/all_gather | solution.py:47
  82.0 4.4 fusion.147
  86.5 14.2 %all-gather.31.cloned.1.call-done = f32[1024,512]{1,0:T(8,128)} async-done(((f32[512,512]{1,0:T(8,128)}), f32[1024,512]{1,0:T(8,128)}) %all-gather.31.cloned.1.call-update) | async-done | bytes 2097168 | tf_op jit(solution)/shard_map/all_gather | solution.py:21
  100.7 2.2 fusion.35
  102.9 4.4 fusion.136
  107.4 12.2 %all-gather.37.cloned.1.call-done = f32[1024,512]{1,0:T(8,128)} async-done(((f32[512,512]{1,0:T(8,128)}), f32[1024,512]{1,0:T(8,128)}) %all-gather.37.cloned.1.call-update) | async-done | bytes 2097168 | tf_op jit(solution)/shard_map/all_gather | solution.py:21
  119.6 2.2 fusion.31
  121.8 4.4 fusion.84
  126.4 46.0 %all-gather.33.cloned.1.call-done = f32[2048,512]{1,0:T(8,128)} async-done(((f32[512,512]{1,0:T(8,128)}), f32[2048,512]{1,0:T(8,128)}) %all-gather.33.cloned.1.call-update) | async-done | bytes 4194320 | tf_op jit(solution)/shard_map/all_gather | solution.py:21
  172.4 2.3 fusion.34
  175.8 3.1 fusion.121
  182.7 2.8 fusion.129
  186.0 8.1 %all_gather.91 = f32[2,512]{1,0:T(2,128)S(1)} all-gather(f32[2,128]{1,0:T(2,128)S(1)} %bitcast.347), channel_id=1, replica_groups=mesh['tm_0'=8,'tm_1'=4,'tm_2'=2,'blk'=4] {'blk'}, dimensions={1}, use_global_device_ids=true | all-gather | bytes 5120 | tf_op jit(solution)/shard_map/all_gather | solution.py:48
  194.1 2.2 fusion.144
  196.3 2.2 fusion.141
  198.5 4.2 all-gather.12
  203.6 21.6 %all-gather.39.cloned.1.call-done = f32[2048,512]{1,0:T(8,128)} async-done(((f32[512,512]{1,0:T(8,128)}), f32[2048,512]{1,0:T(8,128)}) %all-gather.39.cloned.1.call-update) | async-done | bytes 4194320 | tf_op jit(solution)/shard_map/all_gather | solution.py:21
  225.2 2.3 fusion.30
  228.5 3.1 fusion.69
  235.5 2.8 fusion.77
  238.4 2.5 fusion.134
  240.9 2.3 fusion.138
  243.2 9.4 %all-gather.13 = f32[4,1,512]{2,1,0:T(1,128)S(1)} all-gather(f32[1,1,512]{2,1,0:T(1,128)S(1)} %bitcast.331), channel_id=6, replica_groups=mesh['tm_0'=8,'tm_1'=4,'tm_2'=2,'blk'=4] {'tm_1'}, dimensions={0}, use_global_device_ids=true | all-gather | bytes 10240 | tf_op jit(solution)/shard_map/all_gather | solution.py:21
  253.0 2.2 fusion.82
  261.7 22.3 %all-gather.14 = f32[8,1,512]{2,1,0:T(1,128)S(1)} all-gather(f32[1,1,512]{2,1,0:T(1,128)S(1)} %bitcast.342), channel_id=7, replica_groups=mesh['tm_0'=8,'tm_1'=4,'tm_2'=2,'blk'=4] {'tm_0'}, dimensions={0}, use_global_device_ids=true | all-gather | bytes 18432 | tf_op jit(solution)/shard_map/all_gather | solution.py:21
  284.0 2.4 fusion.67
  287.4 3.0 fusion.6
  290.4 3.0 fusion.20
  293.4 28.4 %all-gather.35.cloned.1.call-done = f32[4096,512]{1,0:T(8,128)} async-done(((f32[512,512]{1,0:T(8,128)}), f32[4096,512]{1,0:T(8,128)}) %all-gather.35.cloned.1.call-update) | async-done | bytes 8388624 | tf_op jit(solution)/shard_map/all_gather | solution.py:21
  321.8 2.3 fusion.89
  324.1 2.3 fusion.93
  326.5 2.5 fusion.97
  329.0 2.2 fusion.101
  331.2 2.2 fusion.105
  333.4 2.3 fusion.109
  335.8 2.2 fusion.113
  338.0 2.2 fusion.116
  342.4 1.9 fusion.91
  344.3 1.9 fusion.95
  346.1 1.9 fusion.99
  348.0 1.9 fusion.103
  349.9 1.9 fusion.107
  351.7 1.9 fusion.111
  353.6 2.3 convolution_select_fusion.1
  361.3 8.5 %all_gather.105 = f32[2,512]{1,0:T(2,128)S(1)} all-gather(f32[2,128]{1,0:T(2,128)S(1)} %bitcast.346), channel_id=1, replica_groups=mesh['tm_0'=8,'tm_1'=4,'tm_2'=2,'blk'=4] {'blk'}, dimensions={1}, use_global_device_ids=true | all-gather | bytes 5120 | tf_op jit(solution)/shard_map/all_gather | solution.py:68
  370.8 3.6 all-gather.15
  375.4 9.5 %all-gather.16 = f32[4,1,512]{2,1,0:T(1,128)S(1)} all-gather(f32[1,1,512]{2,1,0:T(1,128)S(1)} %bitcast.330), channel_id=12, replica_groups=mesh['tm_0'=8,'tm_1'=4,'tm_2'=2,'blk'=4] {'tm_1'}, dimensions={0}, use_global_device_ids=true | all-gather | bytes 10240 | tf_op jit(solution)/shard_map/all_gather | solution.py:21
  387.9 19.5 %all-gather.17 = f32[8,1,512]{2,1,0:T(1,128)S(1)} all-gather(f32[1,1,512]{2,1,0:T(1,128)S(1)} %bitcast.339), channel_id=13, replica_groups=mesh['tm_0'=8,'tm_1'=4,'tm_2'=2,'blk'=4] {'tm_0'}, dimensions={0}, use_global_device_ids=true | all-gather | bytes 18432 | tf_op jit(solution)/shard_map/all_gather | solution.py:21
  408.7 7.8 %all-gather.41.cloned.1.call-done = f32[4096,512]{1,0:T(8,128)} async-done(((f32[512,512]{1,0:T(8,128)}), f32[4096,512]{1,0:T(8,128)}) %all-gather.41.cloned.1.call-update) | async-done | bytes 8388624 | tf_op jit(solution)/shard_map/all_gather | solution.py:21
  416.5 2.3 fusion.37
  418.8 2.3 fusion.41
  421.2 2.5 fusion.45
  423.7 2.2 fusion.49
  426.0 2.2 fusion.53
  428.2 2.2 fusion.57
  430.4 2.2 fusion.61
  432.6 2.2 fusion.64
  438.7 1.9 fusion.43
  440.6 2.0 fusion.47
  444.5 1.9 fusion.55
  446.3 1.9 fusion.59
  448.2 2.1 convolution_select_fusion
  (174 shorter events, 45.8 us)
Async XLA Ops:
  7.2 353.7 %copy-start = (f32[2,128,512]{2,1,0:T(8,128)S(1)}, f32[2,128,512]{2,1,0:T(8,128)}, u32[]{:S(2)}) copy-start(f32[2,128,512]{2,1,0:T(8,128)} %param.11) | copy-start | bytes 1572868
  7.2 39.6 %all-gather.27.cloned.1.call-start = ((), (), s32[]{:S(2)}) async-start(), calls=%async_computation | async-start | bytes 2621440 | tf_op jit(solution)/shard_map/all_gather | solution.py:46
  7.9 74.1 %all-gather.29.cloned.1.call-start = ((), (), s32[]{:S(2)}) async-start(), calls=%async_computation.1 | async-start | bytes 2621440 | tf_op jit(solution)/shard_map/all_gather | solution.py:47
  8.7 92.0 %all-gather.31.cloned.1.call-start = ((), (), s32[]{:S(2)}) async-start(), calls=%async_computation.2 | async-start | bytes 3145728 | tf_op jit(solution)/shard_map/all_gather | solution.py:21
  51.2 68.4 %all-gather.37.cloned.1.call-start = ((), (), s32[]{:S(2)}) async-start(), calls=%async_computation.5 | async-start | bytes 3145728 | tf_op jit(solution)/shard_map/all_gather | solution.py:21
  86.4 86.0 %all-gather.33.cloned.1.call-start = ((), (), s32[]{:S(2)}) async-start(), calls=%async_computation.3 | async-start | bytes 5242880 | tf_op jit(solution)/shard_map/all_gather | solution.py:21
  102.9 23.3 %copy-start.13 = (f32[512,512]{1,0:T(8,128)}, f32[512,512]{1,0:T(8,128)S(1)}, u32[]{:S(2)}) copy-start(f32[512,512]{1,0:T(8,128)S(1)} %fusion.35) | copy-start | bytes 3145732
  107.3 117.9 %all-gather.39.cloned.1.call-start = ((), (), s32[]{:S(2)}) async-start(), calls=%async_computation.6 | async-start | bytes 5242880 | tf_op jit(solution)/shard_map/all_gather | solution.py:21
  121.8 53.0 %copy-start.16 = (f32[512,512]{1,0:T(8,128)}, f32[512,512]{1,0:T(8,128)S(1)}, u32[]{:S(2)}) copy-start(f32[512,512]{1,0:T(8,128)S(1)} %fusion.31) | copy-start | bytes 3145732
  126.2 195.6 %all-gather.35.cloned.1.call-start = ((), (), s32[]{:S(2)}) async-start(), calls=%async_computation.4 | async-start | bytes 9437184 | tf_op jit(solution)/shard_map/all_gather | solution.py:21
  172.4 7.4 %copy-start.7 = (f32[2048,512]{1,0:T(8,128)S(1)}, f32[2048,512]{1,0:T(8,128)}, u32[]{:S(2)}) copy-start(f32[2048,512]{1,0:T(8,128)} %all-gather.33.cloned.1.call-done) | copy-start | bytes 12582916
  174.8 1.0 copy-start.26
  178.8 1.0 copy-start.9
  179.8 5.8 %copy-start.34 = (f32[2,128,128]{2,1,0:T(8,128)S(1)}, f32[2,128,128]{2,1,0:T(8,128)}, u32[]{:S(2)}) copy-start(f32[2,128,128]{2,1,0:T(8,128)} %param.12) | copy-start | bytes 393220
  179.8 5.8 %copy-start.37 = (f32[2,128]{1,0:T(2,128)S(1)}, f32[2,128]{1,0:T(2,128)}, u32[]{:S(2)}) copy-start(f32[2,128]{1,0:T(2,128)} %param.13) | copy-start | bytes 3076
  179.8 22.9 %copy-start.3 = (f32[2,512,512]{2,1,0:T(8,128)S(1)}, f32[2,512,512]{2,1,0:T(8,128)}, u32[]{:S(2)}) copy-start(f32[2,512,512]{2,1,0:T(8,128)} %all-gather.29.cloned.1.call-done) | copy-start | bytes 6291460
  181.7 1.0 copy-start.11
  185.6 231.0 %all-gather.41.cloned.1.call-start = ((), (), s32[]{:S(2)}) async-start(), calls=%async_computation.7 | async-start | bytes 9437184 | tf_op jit(solution)/shard_map/all_gather | solution.py:21
  225.2 7.4 %copy-start.5 = (f32[2048,512]{1,0:T(8,128)S(1)}, f32[2048,512]{1,0:T(8,128)}, u32[]{:S(2)}) copy-start(f32[2048,512]{1,0:T(8,128)} %all-gather.39.cloned.1.call-done) | copy-start | bytes 12582916
  227.5 1.0 copy-start.28
  231.6 1.0 copy-start.19
  234.4 1.0 copy-start.21
  238.3 16.9 %copy-start.14 = (f32[512,512]{1,0:T(8,128)S(1)}, f32[512,512]{1,0:T(8,128)}, u32[]{:S(2)}) copy-start(f32[512,512]{1,0:T(8,128)} %copy-done.13) | copy-start | bytes 3145732
  238.3 16.9 %copy-start.15 = (f32[512,512]{1,0:T(8,128)S(1)}, f32[512,512]{1,0:T(8,128)}, u32[]{:S(2)}) copy-start(f32[512,512]{1,0:T(8,128)} %fusion.136) | copy-start | bytes 3145732
  238.3 18.1 %copy-start.17 = (f32[512,512]{1,0:T(8,128)S(1)}, f32[512,512]{1,0:T(8,128)}, u32[]{:S(2)}) copy-start(f32[512,512]{1,0:T(8,128)} %copy-done.16) | copy-start | bytes 3145732
  238.3 18.1 %copy-start.18 = (f32[512,512]{1,0:T(8,128)S(1)}, f32[512,512]{1,0:T(8,128)}, u32[]{:S(2)}) copy-start(f32[512,512]{1,0:T(8,128)} %fusion.84) | copy-start | bytes 3145732
  240.8 16.8 %copy-start.8 = (f32[2048,512]{1,0:T(8,128)S(1)}, f32[2048,512]{1,0:T(8,128)}, u32[]{:S(2)}) copy-start(f32[2048,512]{1,0:T(8,128)} %all-gather.33.cloned.1.call-done) | copy-start | bytes 12582916
  256.4 31.0 %copy-start.10 = (f32[512,512]{1,0:T(8,128)S(1)}, f32[512,512]{1,0:T(8,128)}, u32[]{:S(2)}) copy-start(f32[512,512]{1,0:T(8,128)} %copy-done.9) | copy-start | bytes 3145732
  256.4 31.0 %copy-start.12 = (f32[512,512]{1,0:T(8,128)S(1)}, f32[512,512]{1,0:T(8,128)}, u32[]{:S(2)}) copy-start(f32[512,512]{1,0:T(8,128)} %copy-done.11) | copy-start | bytes 3145732
  256.4 31.0 %copy-start.25 = (f32[512,512]{1,0:T(8,128)S(1)}, f32[512,512]{1,0:T(8,128)}, u32[]{:S(2)}) copy-start(f32[512,512]{1,0:T(8,128)} %fusion.129) | copy-start | bytes 3145732
  256.4 31.0 %copy-start.27 = (f32[512,512]{1,0:T(8,128)S(1)}, f32[512,512]{1,0:T(8,128)}, u32[]{:S(2)}) copy-start(f32[512,512]{1,0:T(8,128)} %copy-done.26) | copy-start | bytes 3145732
  257.6 32.8 %copy-start.31 = (f32[512,512]{1,0:T(8,128)}, f32[512,512]{1,0:T(8,128)S(1)}, u32[]{:S(2)}) copy-start(f32[512,512]{1,0:T(8,128)S(1)} %fusion.15) | copy-start | bytes 3145732
  284.0 6.4 %copy-start.20 = (f32[512,512]{1,0:T(8,128)S(1)}, f32[512,512]{1,0:T(8,128)}, u32[]{:S(2)}) copy-start(f32[512,512]{1,0:T(8,128)} %copy-done.19) | copy-start | bytes 3145732
  284.0 6.4 %copy-start.22 = (f32[512,512]{1,0:T(8,128)S(1)}, f32[512,512]{1,0:T(8,128)}, u32[]{:S(2)}) copy-start(f32[512,512]{1,0:T(8,128)} %copy-done.21) | copy-start | bytes 3145732
  284.0 6.4 %copy-start.23 = (f32[512,512]{1,0:T(8,128)S(1)}, f32[512,512]{1,0:T(8,128)}, u32[]{:S(2)}) copy-start(f32[512,512]{1,0:T(8,128)} %fusion.77) | copy-start | bytes 3145732
  284.0 6.4 %copy-start.29 = (f32[512,512]{1,0:T(8,128)S(1)}, f32[512,512]{1,0:T(8,128)}, u32[]{:S(2)}) copy-start(f32[512,512]{1,0:T(8,128)} %copy-done.28) | copy-start | bytes 3145732
  321.8 18.5 %copy-start.30 = (f32[512,512]{1,0:T(8,128)S(1)}, f32[512,512]{1,0:T(8,128)}, u32[]{:S(2)}) copy-start(f32[512,512]{1,0:T(8,128)} %fusion.6) | copy-start | bytes 3145732
  324.1 17.1 %copy-start.2 = (f32[4096,512]{1,0:T(8,128)S(1)}, f32[4096,512]{1,0:T(8,128)}, u32[]{:S(2)}) copy-start(f32[4096,512]{1,0:T(8,128)} %all-gather.35.cloned.1.call-done) | copy-start | bytes 25165828
  353.6 4.2 copy-start.35
  353.6 20.8 %copy-start.33 = (f32[1024,512]{1,0:T(8,128)S(1)}, f32[1024,512]{1,0:T(8,128)}, u32[]{:S(2)}) copy-start(f32[1024,512]{1,0:T(8,128)} %all-gather.37.cloned.1.call-done) | copy-start | bytes 6291460
  355.9 2.9 copy-start.4
  355.9 28.9 %copy-start.6 = (f32[2048,512]{1,0:T(8,128)S(1)}, f32[2048,512]{1,0:T(8,128)}, u32[]{:S(2)}) copy-start(f32[2048,512]{1,0:T(8,128)} %all-gather.39.cloned.1.call-done) | copy-start | bytes 12582916
  358.8 48.9 %copy-start.32 = (f32[512,512]{1,0:T(8,128)S(1)}, f32[512,512]{1,0:T(8,128)}, u32[]{:S(2)}) copy-start(f32[512,512]{1,0:T(8,128)} %copy-done.31) | copy-start | bytes 3145732
  416.5 18.3 %copy-start.24 = (f32[512,512]{1,0:T(8,128)S(1)}, f32[512,512]{1,0:T(8,128)}, u32[]{:S(2)}) copy-start(f32[512,512]{1,0:T(8,128)} %fusion.20) | copy-start | bytes 3145732
  418.8 17.0 %copy-start.1 = (f32[4096,512]{1,0:T(8,128)S(1)}, f32[4096,512]{1,0:T(8,128)}, u32[]{:S(2)}) copy-start(f32[4096,512]{1,0:T(8,128)} %all-gather.41.cloned.1.call-done) | copy-start | bytes 25165828
  448.2 4.0 copy-start.36
Sparse Core Ops, SparseCore 0:
  9.8 36.9 all-gather.26
  48.6 33.3 all-gather.28
  83.8 16.8 all-gather.30
  102.3 17.1 all-gather.36
  121.2 51.1 all-gather.32
  174.1 51.0 all-gather.38
  227.0 94.7 all-gather.34
  323.6 92.9 all-gather.40
where the time goes:
time: 471 us; the launch traced here: 463 us
  waiting for transfers between devices  200 us (42%)
  matrix products  155 us (33%)
  blocking collectives  85.1 us (18%)
  between operations  15.1 us (3%)
  local copies, waits for them, and re-layouts  6.15 us (1%)
    all_gather x6, waiting for transfers between devices, prefix_by_axis(): pieces = jax.tree.map(lambda part: lax.all_gather(part, axis), so_far)  130 us
    dot_general x34, matrix products, chain_combine(): joined_map = jnp.dot(later[0], earlier[0], precision=highest)  74.4 us
    all_gather x6, blocking collectives, prefix_by_axis(): pieces = jax.tree.map(lambda part: lax.all_gather(part, axis), so_far)  68.5 us
    dot_general x34, matrix products, chain_combine(): joined_offset = jnp.dot(later[0], earlier[1], precision=highest) + later[1]  58.5 us
    all_gather x1, waiting for transfers between devices, shards(): lax.all_gather(filter_map, 'blk', axis=1, tiled=True)  38.1 us
    all_gather x1, waiting for transfers between devices, shards(): lax.all_gather(smoother_gain, 'blk', axis=1, tiled=True)  30.8 us
  transfers between devices with their start and end apart: 8, of which 8 were waited for; matrix products, arithmetic and copies ran while one was open for 25% of the time, Pallas kernels for 0%

commit v1 on v0

--- a/solution.py
+++ b/solution.py
@@ -44,7 +44,9 @@
     drive_rows = jnp.einsum("tro,to->tr", obs_gain, observations, precision=highest)
     full_filter, full_gain, drive = (
         lax.all_gather(filter_map, "blk", axis=1, tiled=True),
-        lax.all_gather(smoother_gain, "blk", axis=1, tiled=True),
+        jnp.concatenate(
+            lax.all_to_all(jnp.stack([smoother_gain] * lax.axis_size("blk")), "blk", 0, 0), axis=1
+        ),
         lax.all_gather(drive_rows, "blk", axis=1, tiled=True),
     )
     identity = jnp.eye(width, dtype=jnp.float32)

time: 471 us -> 517 us (1.098)
  the two profiles are of different devices: /device:TPU:1 before, /device:TPU:32 now
where the time goes in v1:
time: 517 us; the launch traced here: 509 us
  waiting for transfers between devices  194 us (38%)
  matrix products  152 us (29%)
  blocking collectives  135 us (26%)
  between operations  15.2 us (3%)
  local copies, waits for them, and re-layouts  10.8 us (2%)
    all_gather x6, waiting for transfers between devices, prefix_by_axis(): pieces = jax.tree.map(lambda part: lax.all_gather(part, axis), so_far)  193 us
    dot_general x34, matrix products, chain_combine(): joined_map = jnp.dot(later[0], earlier[0], precision=highest)  77.5 us
    all_gather x6, blocking collectives, prefix_by_axis(): pieces = jax.tree.map(lambda part: lax.all_gather(part, axis), so_far)  72.7 us
    dot_general x34, matrix products, chain_combine(): joined_offset = jnp.dot(later[0], earlier[1], precision=highest) + later[1]  55.6 us
    all_to_all x1, blocking collectives, shards(): lax.all_to_all(jnp.stack([smoother_gain] * lax.axis_size('blk')), 'blk',...  43 us
  transfers between devices with their start and end apart: 7, of which 7 were waited for; matrix products, arithmetic and copies ran while one was open for 18% of the time, Pallas kernels for 0%

profile of v1, /device:TPU:32, one launch (start us, length us, event | category | flops | bytes accessed | tf_op | source)
XLA Modules:
  0.0 508.6 jit_solution(4291958274437056114)
XLA Ops:
  9.3 43.0 %all_to_all.5 = f32[4,2,128,512]{3,2,1,0:T(8,128)S(1)} all-to-all(f32[4,2,128,512]{3,2,1,0:T(8,128)S(1)} %stack.28), channel_id=1, replica_groups=mesh['tm_0'=8,'tm_1'=4,'tm_2'=2,'blk'=4] {'blk'}, dimensions={0} | all-to-all | bytes 4194304 | tf_op jit(solution)/shard_map/all_to_all | solution.py:48
  53.7 2.8 fusion.193
  56.8 4.4 fusion.142
  61.2 14.1 %all-gather.34.cloned.1.call-done = f32[1024,512]{1,0:T(8,128)} async-done(((f32[512,512]{1,0:T(8,128)}), f32[1024,512]{1,0:T(8,128)}) %all-gather.34.cloned.1.call-update) | async-done | bytes 2097168 | tf_op jit(solution)/shard_map/all_gather | solution.py:21
  75.4 2.2 fusion.31
  78.6 4.0 fusion.84
  82.7 11.8 %all-gather.28.cloned.1.call-done = f32[1024,512]{1,0:T(8,128)} async-done(((f32[512,512]{1,0:T(8,128)}), f32[1024,512]{1,0:T(8,128)}) %all-gather.28.cloned.1.call-update) | async-done | bytes 2097168 | tf_op jit(solution)/shard_map/all_gather | solution.py:21
  94.4 2.2 fusion.35
  97.6 4.1 fusion.136
  101.9 46.2 %all-gather.36.cloned.1.call-done = f32[2048,512]{1,0:T(8,128)} async-done(((f32[512,512]{1,0:T(8,128)}), f32[2048,512]{1,0:T(8,128)}) %all-gather.36.cloned.1.call-update) | async-done | bytes 4194320 | tf_op jit(solution)/shard_map/all_gather | solution.py:21
  148.1 2.3 fusion.30
  151.5 3.1 fusion.69
  158.4 2.8 fusion.77
  161.5 39.4 %all-gather.30.cloned.1.call-done = f32[2048,512]{1,0:T(8,128)} async-done(((f32[512,512]{1,0:T(8,128)}), f32[2048,512]{1,0:T(8,128)}) %all-gather.30.cloned.1.call-update) | async-done | bytes 4194320 | tf_op jit(solution)/shard_map/all_gather | solution.py:21
  200.9 2.3 fusion.34
  204.3 3.1 fusion.121
  211.1 2.9 fusion.129
  214.5 9.9 %all_gather.88 = f32[2,512]{1,0:T(2,128)S(1)} all-gather(f32[2,128]{1,0:T(2,128)S(1)} %bitcast.353), channel_id=1, replica_groups=mesh['tm_0'=8,'tm_1'=4,'tm_2'=2,'blk'=4] {'blk'}, dimensions={1}, use_global_device_ids=true | all-gather | bytes 5120 | tf_op jit(solution)/shard_map/all_gather | solution.py:50
  224.3 2.2 fusion.162
  228.5 2.2 all-gather.12
  230.7 2.2 fusion.82
  236.2 10.4 %all-gather.13 = f32[4,1,512]{2,1,0:T(1,128)S(1)} all-gather(f32[1,1,512]{2,1,0:T(1,128)S(1)} %bitcast.338), channel_id=6, replica_groups=mesh['tm_0'=8,'tm_1'=4,'tm_2'=2,'blk'=4] {'tm_1'}, dimensions={0}, use_global_device_ids=true | all-gather | bytes 10240 | tf_op jit(solution)/shard_map/all_gather | solution.py:21
  248.2 2.4 fusion.67
  250.6 3.0 fusion.20
  257.6 23.5 %all-gather.14 = f32[8,1,512]{2,1,0:T(1,128)S(1)} all-gather(f32[1,1,512]{2,1,0:T(1,128)S(1)} %bitcast.348), channel_id=7, replica_groups=mesh['tm_0'=8,'tm_1'=4,'tm_2'=2,'blk'=4] {'tm_0'}, dimensions={0}, use_global_device_ids=true | all-gather | bytes 18432 | tf_op jit(solution)/shard_map/all_gather | solution.py:21
  282.1 3.0 fusion.6
  285.2 10.1 %all-gather.38.cloned.1.call-done = f32[4096,512]{1,0:T(8,128)} async-done(((f32[512,512]{1,0:T(8,128)}), f32[4096,512]{1,0:T(8,128)}) %all-gather.38.cloned.1.call-update) | async-done | bytes 8388624 | tf_op jit(solution)/shard_map/all_gather | solution.py:21
  295.3 2.3 fusion.37
  297.6 2.5 fusion.29
  300.2 3.1 fusion.39
  303.2 3.1 fusion.43
  306.3 1.9 fusion.47
  308.2 1.9 fusion.51
  310.1 2.1 fusion.55
  312.1 1.9 fusion.59
  314.0 2.1 convolution_select_fusion
  316.1 1.9 fusion.194
  319.0 71.0 %all-gather.32.cloned.1.call-done = f32[4096,512]{1,0:T(8,128)} async-done(((f32[512,512]{1,0:T(8,128)}), f32[4096,512]{1,0:T(8,128)}) %all-gather.32.cloned.1.call-update) | async-done | bytes 8388624 | tf_op jit(solution)/shard_map/all_gather | solution.py:21
  390.0 2.3 fusion.89
  392.3 2.3 fusion.93
  394.7 2.5 fusion.97
  397.2 2.2 fusion.101
  399.5 2.2 fusion.105
  401.7 2.2 fusion.109
  403.9 2.6 fusion.113
  406.5 2.2 fusion.116
  410.8 1.9 fusion.91
  412.6 1.9 fusion.95
  414.5 1.9 fusion.99
  416.3 1.9 fusion.103
  418.2 1.9 fusion.107
  420.1 2.0 fusion.111
  422.1 2.1 convolution_select_fusion.1
  424.3 1.9 fusion.188
  429.6 9.7 %all_gather.101 = f32[2,512]{1,0:T(2,128)S(1)} all-gather(f32[2,128]{1,0:T(2,128)S(1)} %bitcast.352), channel_id=1, replica_groups=mesh['tm_0'=8,'tm_1'=4,'tm_2'=2,'blk'=4] {'blk'}, dimensions={1}, use_global_device_ids=true | all-gather | bytes 5120 | tf_op jit(solution)/shard_map/all_gather | solution.py:70
  443.2 11.3 %all-gather.16 = f32[4,1,512]{2,1,0:T(1,128)S(1)} all-gather(f32[1,1,512]{2,1,0:T(1,128)S(1)} %bitcast.337), channel_id=12, replica_groups=mesh['tm_0'=8,'tm_1'=4,'tm_2'=2,'blk'=4] {'tm_1'}, dimensions={0}, use_global_device_ids=true | all-gather | bytes 10240 | tf_op jit(solution)/shard_map/all_gather | solution.py:21
  458.6 23.3 %all-gather.17 = f32[8,1,512]{2,1,0:T(1,128)S(1)} all-gather(f32[1,1,512]{2,1,0:T(1,128)S(1)} %bitcast.344), channel_id=13, replica_groups=mesh['tm_0'=8,'tm_1'=4,'tm_2'=2,'blk'=4] {'tm_0'}, dimensions={0}, use_global_device_ids=true | all-gather | bytes 18432 | tf_op jit(solution)/shard_map/all_gather | solution.py:21
  481.9 2.3 fusion.41
  484.2 2.2 fusion.45
  486.4 2.2 fusion.49
  488.7 2.2 fusion.53
  490.9 2.2 fusion.57
  493.1 2.2 fusion.61
  495.3 2.2 fusion.64
  (184 shorter events, 46.3 us)
Async XLA Ops:
  7.2 422.0 %copy-start = (f32[2,128,512]{2,1,0:T(8,128)S(1)}, f32[2,128,512]{2,1,0:T(8,128)}, u32[]{:S(2)}) copy-start(f32[2,128,512]{2,1,0:T(8,128)} %param.11) | copy-start | bytes 1572868
  7.2 49.6 %all-gather.26.cloned.1.call-start = ((), (), s32[]{:S(2)}) async-start(), calls=%async_computation.1 | async-start | bytes 2621440 | tf_op jit(solution)/shard_map/all_gather | solution.py:46
  7.9 67.5 %all-gather.34.cloned.1.call-start = ((), (), s32[]{:S(2)}) async-start(), calls=%async_computation.5 | async-start | bytes 3145728 | tf_op jit(solution)/shard_map/all_gather | solution.py:21
  52.4 1.0 copy-start.8
  52.4 1.3 copy-start.10
  56.6 37.9 %all-gather.28.cloned.1.call-start = ((), (), s32[]{:S(2)}) async-start(), calls=%async_computation.2 | async-start | bytes 3145728 | tf_op jit(solution)/shard_map/all_gather | solution.py:21
  61.2 86.9 %all-gather.36.cloned.1.call-start = ((), (), s32[]{:S(2)}) async-start(), calls=%async_computation.6 | async-start | bytes 5242880 | tf_op jit(solution)/shard_map/all_gather | solution.py:21
  77.6 1.0 copy-start.23
  82.6 118.3 %all-gather.30.cloned.1.call-start = ((), (), s32[]{:S(2)}) async-start(), calls=%async_computation.3 | async-start | bytes 5242880 | tf_op jit(solution)/shard_map/all_gather | solution.py:21
  96.6 1.0 copy-start.16
  101.7 193.6 %all-gather.38.cloned.1.call-start = ((), (), s32[]{:S(2)}) async-start(), calls=%async_computation.7 | async-start | bytes 9437184 | tf_op jit(solution)/shard_map/all_gather | solution.py:21
  148.1 7.3 %copy-start.4 = (f32[2048,512]{1,0:T(8,128)S(1)}, f32[2048,512]{1,0:T(8,128)}, u32[]{:S(2)}) copy-start(f32[2048,512]{1,0:T(8,128)} %all-gather.36.cloned.1.call-done) | copy-start | bytes 12582916
  150.5 1.0 copy-start.32
  154.5 1.0 copy-start.19
  157.3 1.0 copy-start.21
  161.3 228.8 %all-gather.32.cloned.1.call-start = ((), (), s32[]{:S(2)}) async-start(), calls=%async_computation.4 | async-start | bytes 9437184 | tf_op jit(solution)/shard_map/all_gather | solution.py:21
  200.9 7.4 %copy-start.6 = (f32[2048,512]{1,0:T(8,128)S(1)}, f32[2048,512]{1,0:T(8,128)}, u32[]{:S(2)}) copy-start(f32[2048,512]{1,0:T(8,128)} %all-gather.30.cloned.1.call-done) | copy-start | bytes 12582916
  203.3 1.0 copy-start.30
  207.3 1.0 copy-start.12
  208.3 5.8 %copy-start.39 = (f32[2,128,128]{2,1,0:T(8,128)S(1)}, f32[2,128,128]{2,1,0:T(8,128)}, u32[]{:S(2)}) copy-start(f32[2,128,128]{2,1,0:T(8,128)} %param.12) | copy-start | bytes 393220
  208.3 5.8 %copy-start.42 = (f32[2,128]{1,0:T(2,128)S(1)}, f32[2,128]{1,0:T(2,128)}, u32[]{:S(2)}) copy-start(f32[2,128]{1,0:T(2,128)} %param.13) | copy-start | bytes 3076
  208.3 18.2 %copy-start.3 = (f32[2,512,512]{2,1,0:T(8,128)S(1)}, f32[2,512,512]{2,1,0:T(8,128)}, u32[]{:S(2)}) copy-start(f32[2,512,512]{2,1,0:T(8,128)} %all-gather.26.cloned.1.call-done) | copy-start | bytes 6291460
  210.2 1.0 copy-start.14
  214.1 18.8 %copy-start.24 = (f32[512,512]{1,0:T(8,128)S(1)}, f32[512,512]{1,0:T(8,128)}, u32[]{:S(2)}) copy-start(f32[512,512]{1,0:T(8,128)} %copy-done.23) | copy-start | bytes 3145732
  214.1 18.8 %copy-start.25 = (f32[512,512]{1,0:T(8,128)S(1)}, f32[512,512]{1,0:T(8,128)}, u32[]{:S(2)}) copy-start(f32[512,512]{1,0:T(8,128)} %fusion.84) | copy-start | bytes 3145732
  214.1 20.0 %copy-start.38 = (f32[1024,512]{1,0:T(8,128)S(1)}, f32[1024,512]{1,0:T(8,128)}, u32[]{:S(2)}) copy-start(f32[1024,512]{1,0:T(8,128)} %all-gather.28.cloned.1.call-done) | copy-start | bytes 6291460
  226.5 20.5 %copy-start.17 = (f32[512,512]{1,0:T(8,128)S(1)}, f32[512,512]{1,0:T(8,128)}, u32[]{:S(2)}) copy-start(f32[512,512]{1,0:T(8,128)} %copy-done.16) | copy-start | bytes 3145732
  226.5 20.5 %copy-start.18 = (f32[512,512]{1,0:T(8,128)S(1)}, f32[512,512]{1,0:T(8,128)}, u32[]{:S(2)}) copy-start(f32[512,512]{1,0:T(8,128)} %fusion.136) | copy-start | bytes 3145732
  233.0 17.6 %copy-start.20 = (f32[512,512]{1,0:T(8,128)S(1)}, f32[512,512]{1,0:T(8,128)}, u32[]{:S(2)}) copy-start(f32[512,512]{1,0:T(8,128)} %copy-done.19) | copy-start | bytes 3145732
  233.0 17.6 %copy-start.22 = (f32[512,512]{1,0:T(8,128)S(1)}, f32[512,512]{1,0:T(8,128)}, u32[]{:S(2)}) copy-start(f32[512,512]{1,0:T(8,128)} %copy-done.21) | copy-start | bytes 3145732
  233.0 17.6 %copy-start.29 = (f32[512,512]{1,0:T(8,128)S(1)}, f32[512,512]{1,0:T(8,128)}, u32[]{:S(2)}) copy-start(f32[512,512]{1,0:T(8,128)} %fusion.77) | copy-start | bytes 3145732
  233.0 17.6 %copy-start.33 = (f32[512,512]{1,0:T(8,128)S(1)}, f32[512,512]{1,0:T(8,128)}, u32[]{:S(2)}) copy-start(f32[512,512]{1,0:T(8,128)} %copy-done.32) | copy-start | bytes 3145732
  234.2 19.4 %copy-start.35 = (f32[512,512]{1,0:T(8,128)}, f32[512,512]{1,0:T(8,128)S(1)}, u32[]{:S(2)}) copy-start(f32[512,512]{1,0:T(8,128)S(1)} %fusion.15) | copy-start | bytes 3145732
  248.2 5.4 %copy-start.7 = (f32[2048,512]{1,0:T(8,128)S(1)}, f32[2048,512]{1,0:T(8,128)}, u32[]{:S(2)}) copy-start(f32[2048,512]{1,0:T(8,128)} %all-gather.30.cloned.1.call-done) | copy-start | bytes 12582916
  253.5 28.5 %copy-start.13 = (f32[512,512]{1,0:T(8,128)S(1)}, f32[512,512]{1,0:T(8,128)}, u32[]{:S(2)}) copy-start(f32[512,512]{1,0:T(8,128)} %copy-done.12) | copy-start | bytes 3145732
  253.5 28.5 %copy-start.15 = (f32[512,512]{1,0:T(8,128)S(1)}, f32[512,512]{1,0:T(8,128)}, u32[]{:S(2)}) copy-start(f32[512,512]{1,0:T(8,128)} %copy-done.14) | copy-start | bytes 3145732
  253.5 28.5 %copy-start.28 = (f32[512,512]{1,0:T(8,128)S(1)}, f32[512,512]{1,0:T(8,128)}, u32[]{:S(2)}) copy-start(f32[512,512]{1,0:T(8,128)} %fusion.129) | copy-start | bytes 3145732
  253.6 28.5 %copy-start.31 = (f32[512,512]{1,0:T(8,128)S(1)}, f32[512,512]{1,0:T(8,128)}, u32[]{:S(2)}) copy-start(f32[512,512]{1,0:T(8,128)} %copy-done.30) | copy-start | bytes 3145732
  295.3 11.1 %copy-start.1 = (f32[4096,512]{1,0:T(8,128)S(1)}, f32[4096,512]{1,0:T(8,128)}, u32[]{:S(2)}) copy-start(f32[4096,512]{1,0:T(8,128)} %all-gather.38.cloned.1.call-done) | copy-start | bytes 25165828
  314.0 2.1 copy-start.26
  314.0 4.0 copy-start.40
  390.0 18.7 %copy-start.34 = (f32[512,512]{1,0:T(8,128)S(1)}, f32[512,512]{1,0:T(8,128)}, u32[]{:S(2)}) copy-start(f32[512,512]{1,0:T(8,128)} %fusion.6) | copy-start | bytes 3145732
  392.3 17.4 %copy-start.2 = (f32[4096,512]{1,0:T(8,128)S(1)}, f32[4096,512]{1,0:T(8,128)}, u32[]{:S(2)}) copy-start(f32[4096,512]{1,0:T(8,128)} %all-gather.32.cloned.1.call-done) | copy-start | bytes 25165828
  422.1 4.0 copy-start.41
  424.2 15.1 %copy-start.9 = (f32[1,4,128,512]{3,2,0,1:T(8,128)S(1)}, f32[1,4,128,512]{3,2,0,1:T(8,128)}, u32[]{:S(2)}) copy-start(f32[1,4,128,512]{3,2,0,1:T(8,128)} %copy-done.8) | copy-start | bytes 3145732
  424.2 18.0 %copy-start.37 = (f32[1024,512]{1,0:T(8,128)S(1)}, f32[1024,512]{1,0:T(8,128)}, u32[]{:S(2)}) copy-start(f32[1024,512]{1,0:T(8,128)} %all-gather.34.cloned.1.call-done) | copy-start | bytes 6291460
  424.3 30.3 %copy-start.5 = (f32[2048,512]{1,0:T(8,128)S(1)}, f32[2048,512]{1,0:T(8,128)}, u32[]{:S(2)}) copy-start(f32[2048,512]{1,0:T(8,128)} %all-gather.36.cloned.1.call-done) | copy-start | bytes 12582916
  427.1 30.5 %copy-start.36 = (f32[512,512]{1,0:T(8,128)S(1)}, f32[512,512]{1,0:T(8,128)}, u32[]{:S(2)}) copy-start(f32[512,512]{1,0:T(8,128)} %copy-done.35) | copy-start | bytes 3145732
  457.6 40.0 %copy-start.27 = (f32[512,512]{1,0:T(8,128)S(1)}, f32[512,512]{1,0:T(8,128)}, u32[]{:S(2)}) copy-start(f32[512,512]{1,0:T(8,128)} %fusion.20) | copy-start | bytes 3145732
  481.9 17.0 %copy-start.11 = (f32[1,4,128,512]{3,2,0,1:T(8,128)S(1)}, f32[1,4,128,512]{3,2,0,1:T(8,128)}, u32[]{:S(2)}) copy-start(f32[1,4,128,512]{3,2,0,1:T(8,128)} %copy-done.10) | copy-start | bytes 3145732
Sparse Core Ops, SparseCore 0:
  9.8 46.9 all-gather.25
  58.6 16.7 all-gather.33
  77.2 17.1 all-gather.27
  96.1 52.0 all-gather.35
  149.8 51.0 all-gather.29
  202.6 92.6 all-gather.37
  297.1 92.9 all-gather.31
